TPU v7x, 512 devices: a whole 4x8x8 slice. The times are simulated.
512 devices in a mesh: tp: 8 (over y), row: 8 (over z_hi, x), col: 8 (over z_lo, core).
Axes of the slice: x: 4, y: 8, z: 8 (z_hi: 2, z_lo: 4; z = z_hi * 4 + z_lo), core: 2. Of those that a mesh axis runs over, the one named last changes fastest.
Arguments:
- hidden: bfloat16 [128, 14336], P('col', 'row'), may hold values from -6 to 6
- out_grad: bfloat16 [128, 4096], P(None, ('tp', 'row')), may hold values from -6 to 6
- basis_in: bfloat16 [14336, 4096], P(('row', 'col'), 'tp'), may hold values from -0.046875 to 0.046875
- basis_out: bfloat16 [4096, 1024], P(('tp', 'row'), 'col'), may hold values from -0.09375 to 0.09375
- eigen: float32 [4096, 1024], P(('tp', 'row'), 'col'), may hold values from 0.02 to 2
Outputs:
- precond: float32 [4096, 14336], P(('tp', 'col'), 'row')
All inputs are finite; a program needn't handle non-finite values.
Results may differ from a plain program's by a relative error of at most 0.024.
Values may be sent and summed in bfloat16 or wider, within the bound.
A program may use at most 64 MiB of HBM per device.

v0:
```python
import jax
import jax.numpy as jnp
from jax import lax
from jax.sharding import PartitionSpec as P

damping = 0.01


def sent_to_all(array, axis):
    devices = lax.axis_size(axis)
    return lax.all_to_all(
        jnp.broadcast_to(array[None], (devices, *array.shape)), axis, 0, 0, tiled=True
    )


def laid_out(tiles, dim):
    dims = list(tiles.shape[1:])
    dims[dim] *= tiles.shape[0]
    return jnp.moveaxis(tiles, 0, dim).reshape(dims)


def gathered_copies(array, axis, dim):
    tiles = sent_to_all(array, axis)
    return laid_out(tiles, dim)


def in_blocks(array, dim, devices):
    before, after = (array.shape[:dim], array.shape[dim + 1 :])
    return jnp.moveaxis(array.reshape(*before, devices, -1, *after), dim, 0)


def sent_and_summed(array, axis, dim):
    tiles = in_blocks(array, dim, lax.axis_size(axis))
    arrived = lax.all_to_all(tiles, axis, split_axis=0, concat_axis=0, tiled=True)
    return arrived.astype(jnp.float32).sum(axis=0)


def contract_rows(left, right):
    return lax.dot_general(
        left, right, (((0,), (0,)), ((), ())), preferred_element_type=jnp.float32
    )


def contract_cols(left, right):
    return lax.dot_general(
        left, right, (((1,), (1,)), ((), ())), preferred_element_type=jnp.float32
    )


def shards(hidden, out_grad, basis_in, basis_out, eigen):
    tp_count = lax.axis_size("tp")
    col_count = lax.axis_size("col")
    basis_block = gathered_copies(basis_in, "col", 0)
    partial_in = jnp.dot(hidden, basis_block, preferred_element_type=jnp.float32)
    rotated_in = sent_and_summed(partial_in.astype(jnp.bfloat16), "row", 1).astype(jnp.bfloat16)
    rotated_in = gathered_copies(rotated_in, "col", 0)
    queries = rotated_in.shape[0]
    out_rows = gathered_copies(basis_out, ("tp", "row"), 0)
    grad_full = lax.all_gather(out_grad, ("tp", "row"), axis=1, tiled=True)
    rotated_out = jnp.dot(grad_full, out_rows, preferred_element_type=jnp.float32).astype(
        jnp.bfloat16
    )
    coeff = contract_rows(rotated_in, rotated_out)
    scaled = (coeff / (queries * (eigen + damping))).astype(jnp.bfloat16)
    mixed_part = contract_cols(scaled, out_rows)
    depth = mixed_part.shape[0]
    width = mixed_part.shape[1]
    mixed_part = mixed_part.reshape(depth, tp_count, col_count, width // (tp_count * col_count))
    mixed = sent_and_summed(mixed_part.astype(jnp.bfloat16), "col", 2)
    mixed = mixed.reshape(depth, width // col_count).astype(jnp.bfloat16)
    mixed = gathered_copies(mixed, "row", 0)
    return sent_and_summed(
        lax.dot_general(
            mixed, basis_block, (((0,), (1,)), ((), ())), preferred_element_type=jnp.float32
        ).astype(jnp.bfloat16),
        "tp",
        0,
    )


def solution(mesh):
    placed = (
        P("col", "row"),
        P(None, ("tp", "row")),
        P(("row", "col"), "tp"),
        P(("tp", "row"), "col"),
        P(("tp", "row"), "col"),
    )
    return jax.shard_map(
        shards, mesh=mesh, in_specs=placed, out_specs=P(("tp", "col"), "row"), check_vma=False
    )
```

profile of v0, /device:TPU:8, one launch (start us, length us, event | category | flops | bytes accessed | tf_op | source)
XLA Modules:
  0.0 334.7 jit_solution(7538081881652696159)
XLA Ops:
  6.5 1.1 broadcast_in_dim.8
  7.6 50.5 %all_to_all.35 = bf16[8,224,512]{2,1,0:T(8,128)(2,1)S(1)} all-to-all(bf16[8,224,512]{2,1,0:T(8,128)(2,1)S(1)} %broadcast_in_dim.8), channel_id=1, replica_groups=mesh['tp'=8,'row'=8,'col'=8] {'col'}, dimensions={0} | all-to-all | bytes 3670016 | tf_op jit(solution)/shard_map/all_to_all | solution.py:11
  58.1 0.3 convolution_convert_fusion.3
  58.5 0.1 reshape.37
  58.6 0.1 reshape.44
  58.7 20.0 %all_to_all.36 = bf16[8,2,512]{2,1,0:T(2,128)(2,1)S(1)} all-to-all(bf16[8,2,512]{2,1,0:T(2,128)(2,1)S(1)} %reshape.44), channel_id=1, replica_groups=mesh['tp'=8,'row'=8,'col'=8] {'row'}, dimensions={0} | all-to-all | bytes 32768 | tf_op jit(solution)/shard_map/all_to_all | solution.py:34
  78.8 0.1 reshape.46
  78.9 8.0 %all_to_all.37 = bf16[8,2,512]{2,1,0:T(2,128)(2,1)S(1)} all-to-all(bf16[8,2,512]{2,1,0:T(2,128)(2,1)S(1)} %reshape.46), channel_id=1, replica_groups=mesh['tp'=8,'row'=8,'col'=8] {'col'}, dimensions={0} | all-to-all | bytes 32768 | tf_op jit(solution)/shard_map/all_to_all | solution.py:11
  86.9 1.3 broadcast_in_dim.10
  88.2 8.8 %all-to-all-start.3 = ((bf16[64,64,128]{2,1,0:T(8,128)(2,1)}), bf16[64,64,128]{2,1,0:T(8,128)(2,1)S(1)}, u32[]{:S(2)}, u32[]{:S(2)}) async-start(bf16[64,64,128]{2,1,0:T(8,128)(2,1)} %broadcast_in_dim.10), calls=%async_computation.3 | async-start | bytes 2097152 | tf_op jit(solution)/shard_map/all_to_all | solution.py:11
  97.0 0.7 all-gather.2.cloned.1.call-update
  97.8 30.5 %all-to-all-done.3 = bf16[64,64,128]{2,1,0:T(8,128)(2,1)S(1)} async-done(((bf16[64,64,128]{2,1,0:T(8,128)(2,1)}), bf16[64,64,128]{2,1,0:T(8,128)(2,1)S(1)}, u32[]{:S(2)}, u32[]{:S(2)}) %all-to-all-start.3) | async-done | bytes 1048608 | tf_op jit(solution)/shard_map/all_to_all | solution.py:11
  128.3 104.7 %all-gather.2.cloned.1.call-done = bf16[128,4096]{0,1:T(8,128)(2,1)} async-done(((bf16[128,64]{0,1:T(8,128)(2,1)}), bf16[128,4096]{0,1:T(8,128)(2,1)}) %all-gather.2.cloned.1.call-update) | async-done | bytes 1048592 | tf_op jit(solution)/shard_map/all_gather | solution.py:59
  233.1 1.8 fusion.4
  234.9 1.1 fusion
  236.1 0.7 reshape.48
  236.8 18.4 %all_to_all.38 = bf16[8,2,16384]{2,1,0:T(2,128)(2,1)} all-to-all(bf16[8,2,16384]{2,1,0:T(2,128)(2,1)S(1)} %reshape.48), channel_id=1, replica_groups=mesh['tp'=8,'row'=8,'col'=8] {'col'}, dimensions={0} | all-to-all | bytes 1048576 | tf_op jit(solution)/shard_map/all_to_all | solution.py:34
  255.3 2.3 reshape.49
  257.6 0.2 bitcast_reduce_fusion
  257.9 0.1 convert_element_type.33
  258.1 20.5 %all_to_all.39 = bf16[8,64,512]{2,1,0:T(8,128)(2,1)S(1)} all-to-all(bf16[8,64,512]{2,1,0:T(8,128)(2,1)S(1)} %broadcast_in_dim.11), channel_id=1, replica_groups=mesh['tp'=8,'row'=8,'col'=8] {'row'}, dimensions={0} | all-to-all | bytes 1048576 | tf_op jit(solution)/shard_map/all_to_all | solution.py:11
  278.5 1.2 convolution_convert_fusion
  279.7 47.1 %all_to_all.40 = bf16[8,64,1792]{2,1,0:T(8,128)(2,1)S(1)} all-to-all(bf16[8,64,1792]{2,1,0:T(8,128)(2,1)S(1)} %bitcast.36), channel_id=1, replica_groups=mesh['tp'=8,'row'=8,'col'=8] {'tp'}, dimensions={0} | all-to-all | bytes 3670016 | tf_op jit(solution)/shard_map/all_to_all | solution.py:34
  326.9 1.0 convert_reduce_fusion
  (15 shorter events, 0.5 us)
Async XLA Ops:
  6.5 51.6 %copy-start = (bf16[16,1792]{1,0:T(8,128)(2,1)S(1)}, bf16[16,1792]{1,0:T(8,128)(2,1)}, u32[]{:S(2)}) copy-start(bf16[16,1792]{1,0:T(8,128)(2,1)} %param.5) | copy-start | bytes 172036
  58.1 28.8 %copy-start.2 = (bf16[64,128]{1,0:T(8,128)(2,1)S(1)}, bf16[64,128]{1,0:T(8,128)(2,1)}, u32[]{:S(2)}) copy-start(bf16[64,128]{1,0:T(8,128)(2,1)} %param.8) | copy-start | bytes 49156
  58.5 174.6 %copy-start.1 = (f32[64,128]{1,0:T(8,128)S(1)}, f32[64,128]{1,0:T(8,128)}, u32[]{:S(2)}) copy-start(f32[64,128]{1,0:T(8,128)} %param.9) | copy-start | bytes 98308
  88.2 40.1 %all-to-all-start.3 = ((bf16[64,64,128]{2,1,0:T(8,128)(2,1)}), bf16[64,64,128]{2,1,0:T(8,128)(2,1)S(1)}, u32[]{:S(2)}, u32[]{:S(2)}) async-start(bf16[64,64,128]{2,1,0:T(8,128)(2,1)} %broadcast_in_dim.10), calls=%async_computation.3 | async-start | bytes 2097152 | tf_op jit(solution)/shard_map/all_to_all | solution.py:11
  97.0 136.1 %all-gather.2.cloned.1.call-start = ((), (), s32[]{:S(2)}) async-start(), calls=%async_computation.7 | async-start | bytes 1064960 | tf_op jit(solution)/shard_map/all_gather | solution.py:59
Sparse Core Ops, SparseCore 0:
  102.1 130.8 all-gather.1
where the time goes:
time: 335 us
  blocking collectives  165 us (49%)
  waiting for transfers between devices  136 us (41%)
  between operations  13.5 us (4%)
  starting transfers between devices  8.8 us (3%)
  local copies, waits for them, and re-layouts  6.28 us (2%)
  matrix products  4.45 us (1%)
    all_gather x1, waiting for transfers between devices, shards(): grad_full = lax.all_gather(out_grad, ('tp', 'row'), axis=1, tiled=True)  105 us
    all_to_all x3, blocking collectives, sent_and_summed(): lax.all_to_all(tiles, axis, split_axis=0, concat_axis=0, tiled=True)  85.5 us
    all_to_all x3, blocking collectives, sent_to_all(): lax.all_to_all(jnp.broadcast_to(array[None], (devices, *array.shape)), ax...  79 us
    all_to_all x1, waiting for transfers between devices, sent_to_all(): lax.all_to_all(jnp.broadcast_to(array[None], (devices, *array.shape)), ax...  30.5 us
    all_to_all x1, starting transfers between devices, sent_to_all(): lax.all_to_all(jnp.broadcast_to(array[None], (devices, *array.shape)), ax...  8.75 us
  transfers between devices with their start and end apart: 2, of which 2 were waited for; matrix products, arithmetic and copies ran while one was open for 0% of the time, Pallas kernels for 0%

commit v1 on v0

--- a/solution.py
+++ b/solution.py
@@ -56,7 +56,8 @@
     rotated_in = gathered_copies(rotated_in, "col", 0)
     queries = rotated_in.shape[0]
     out_rows = gathered_copies(basis_out, ("tp", "row"), 0)
-    grad_full = lax.all_gather(out_grad, ("tp", "row"), axis=1, tiled=True)
+    sent = jnp.stack([out_grad] * lax.axis_size(("tp", "row")))
+    grad_full = jnp.concatenate(lax.all_to_all(sent, ("tp", "row"), 0, 0), axis=1)
     rotated_out = jnp.dot(grad_full, out_rows, preferred_element_type=jnp.float32).astype(
         jnp.bfloat16
     )

time: 335 us -> 256 us (0.76)
  waiting for transfers between devices: 136 us -> 60.9 us
  between operations: 13.5 us -> 0.12 us
  starting transfers between devices: 8.8 us -> 16.4 us
    all_gather x1 -> x0, waiting for transfers between devices: 105 us -> none  [shards(): grad_full = lax.all_gather(out_grad, ('tp', 'row'), axis=1, tiled=True)]
    all_to_all x0 -> x1, waiting for transfers between devices: none -> 31.2 us  [shards(): lax.all_to_all(sent, ('tp', 'row'), 0, 0)]
    all_to_all x0 -> x1, starting transfers between devices: none -> 7.62 us  [shards(): lax.all_to_all(sent, ('tp', 'row'), 0, 0)]
where the time goes in v1:
time: 256 us; the launch traced here: 255 us
  blocking collectives  164 us (64%)
  waiting for transfers between devices  60.9 us (24%)
  starting transfers between devices  16.4 us (6%)
  local copies, waits for them, and re-layouts  7.53 us (3%)
  matrix products  4.45 us (2%)
    all_to_all x3, blocking collectives, sent_and_summed(): lax.all_to_all(tiles, axis, split_axis=0, concat_axis=0, tiled=True)  84.3 us
    all_to_all x3, blocking collectives, sent_to_all(): lax.all_to_all(jnp.broadcast_to(array[None], (devices, *array.shape)), ax...  80.1 us
    all_to_all x1, waiting for transfers between devices, shards(): lax.all_to_all(sent, ('tp', 'row'), 0, 0)  31.2 us
    all_to_all x1, waiting for transfers between devices, sent_to_all(): lax.all_to_all(jnp.broadcast_to(array[None], (devices, *array.shape)), ax...  29.7 us
    all_to_all x1, starting transfers between devices, sent_to_all(): lax.all_to_all(jnp.broadcast_to(array[None], (devices, *array.shape)), ax...  8.75 us
    all_to_all x1, starting transfers between devices, shards(): lax.all_to_all(sent, ('tp', 'row'), 0, 0)  7.62 us
  transfers between devices with their start and end apart: 2, of which 2 were waited for; matrix products, arithmetic and copies ran while one was open for 0% of the time, Pallas kernels for 0%

profile of v1, /device:TPU:8, one launch (start us, length us, event | category | flops | bytes accessed | tf_op | source)
XLA Modules:
  0.0 255.0 jit_solution(4505531096859930628)
XLA Ops:
  0.0 1.1 broadcast_in_dim.8
  1.1 50.5 %all_to_all.40 = bf16[8,224,512]{2,1,0:T(8,128)(2,1)S(1)} all-to-all(bf16[8,224,512]{2,1,0:T(8,128)(2,1)S(1)} %broadcast_in_dim.8), channel_id=1, replica_groups=mesh['tp'=8,'row'=8,'col'=8] {'col'}, dimensions={0} | all-to-all | bytes 3670016 | tf_op jit(solution)/shard_map/all_to_all | solution.py:11
  51.6 0.3 convolution_convert_fusion.2
  51.9 0.1 reshape.41
  52.1 0.1 reshape.49
  52.2 20.0 %all_to_all.41 = bf16[8,2,512]{2,1,0:T(2,128)(2,1)S(1)} all-to-all(bf16[8,2,512]{2,1,0:T(2,128)(2,1)S(1)} %reshape.49), channel_id=1, replica_groups=mesh['tp'=8,'row'=8,'col'=8] {'row'}, dimensions={0} | all-to-all | bytes 32768 | tf_op jit(solution)/shard_map/all_to_all | solution.py:34
  72.1 1.2 broadcast_in_dim.10
  73.4 8.8 %all-to-all-start.4 = ((bf16[64,64,128]{2,1,0:T(8,128)(2,1)}), bf16[64,64,128]{2,1,0:T(8,128)(2,1)S(1)}, u32[]{:S(2)}, u32[]{:S(2)}) async-start(bf16[64,64,128]{2,1,0:T(8,128)(2,1)} %broadcast_in_dim.10), calls=%async_computation.4 | async-start | bytes 2097152 | tf_op jit(solution)/shard_map/all_to_all | solution.py:11
  82.4 29.7 %all-to-all-done.4 = bf16[64,64,128]{2,1,0:T(8,128)(2,1)S(1)} async-done(((bf16[64,64,128]{2,1,0:T(8,128)(2,1)}), bf16[64,64,128]{2,1,0:T(8,128)(2,1)S(1)}, u32[]{:S(2)}, u32[]{:S(2)}) %all-to-all-start.4) | async-done | bytes 1048608 | tf_op jit(solution)/shard_map/all_to_all | solution.py:11
  112.1 8.4 %all_to_all.42 = bf16[8,2,512]{2,1,0:T(2,128)(2,1)S(1)} all-to-all(bf16[8,2,512]{2,1,0:T(2,128)(2,1)S(1)} %reshape.51), channel_id=1, replica_groups=mesh['tp'=8,'row'=8,'col'=8] {'col'}, dimensions={0} | all-to-all | bytes 32768 | tf_op jit(solution)/shard_map/all_to_all | solution.py:11
  120.5 1.3 stack.2
  121.8 7.6 %all-to-all-start.3 = ((bf16[64,128,64]{1,2,0:T(8,128)(2,1)}), bf16[64,128,64]{1,2,0:T(8,128)(2,1)}, u32[]{:S(2)}, u32[]{:S(2)}) async-start(bf16[64,128,64]{1,2,0:T(8,128)(2,1)} %stack.2), calls=%async_computation.3 | async-start | bytes 2097152 | tf_op jit(solution)/shard_map/all_to_all | solution.py:60
  129.5 31.2 %all-to-all-done.3 = bf16[64,128,64]{1,2,0:T(8,128)(2,1)} async-done(((bf16[64,128,64]{1,2,0:T(8,128)(2,1)}), bf16[64,128,64]{1,2,0:T(8,128)(2,1)}, u32[]{:S(2)}, u32[]{:S(2)}) %all-to-all-start.3) | async-done | bytes 1048608 | tf_op jit(solution)/shard_map/all_to_all | solution.py:60
  160.7 1.8 fusion.5
  162.5 1.1 fusion
  163.7 0.7 reshape.53
  164.5 18.4 %all_to_all.43 = bf16[8,2,16384]{2,1,0:T(2,128)(2,1)} all-to-all(bf16[8,2,16384]{2,1,0:T(2,128)(2,1)S(1)} %reshape.53), channel_id=1, replica_groups=mesh['tp'=8,'row'=8,'col'=8] {'col'}, dimensions={0} | all-to-all | bytes 1048576 | tf_op jit(solution)/shard_map/all_to_all | solution.py:34
  182.9 2.3 reshape.54
  185.2 0.2 bitcast_reduce_fusion
  185.5 0.1 convert_element_type.33
  185.7 21.2 %all_to_all.44 = bf16[8,64,512]{2,1,0:T(8,128)(2,1)S(1)} all-to-all(bf16[8,64,512]{2,1,0:T(8,128)(2,1)S(1)} %broadcast_in_dim.11), channel_id=1, replica_groups=mesh['tp'=8,'row'=8,'col'=8] {'row'}, dimensions={0} | all-to-all | bytes 1048576 | tf_op jit(solution)/shard_map/all_to_all | solution.py:11
  206.9 1.2 convolution_convert_fusion
  208.1 45.9 %all_to_all.45 = bf16[8,64,1792]{2,1,0:T(8,128)(2,1)S(1)} all-to-all(bf16[8,64,1792]{2,1,0:T(8,128)(2,1)S(1)} %bitcast.49), channel_id=1, replica_groups=mesh['tp'=8,'row'=8,'col'=8] {'tp'}, dimensions={0} | all-to-all | bytes 3670016 | tf_op jit(solution)/shard_map/all_to_all | solution.py:34
  254.0 1.0 convert_reduce_fusion
  (17 shorter events, 0.5 us)
Async XLA Ops:
  0.0 51.6 %copy-start = (bf16[16,1792]{1,0:T(8,128)(2,1)S(1)}, bf16[16,1792]{1,0:T(8,128)(2,1)}, u32[]{:S(2)}) copy-start(bf16[16,1792]{1,0:T(8,128)(2,1)} %param.5) | copy-start | bytes 172036
  51.6 20.5 %copy-start.1 = (bf16[64,128]{1,0:T(8,128)(2,1)S(1)}, bf16[64,128]{1,0:T(8,128)(2,1)}, u32[]{:S(2)}) copy-start(bf16[64,128]{1,0:T(8,128)(2,1)} %param.8) | copy-start | bytes 49156
  51.9 68.5 %copy-start.2 = (bf16[128,64]{0,1:T(8,128)(2,1)S(1)}, bf16[128,64]{0,1:T(8,128)(2,1)}, u32[]{:S(2)}) copy-start(bf16[128,64]{0,1:T(8,128)(2,1)} %param.6) | copy-start | bytes 49156
  73.4 38.7 %all-to-all-start.4 = ((bf16[64,64,128]{2,1,0:T(8,128)(2,1)}), bf16[64,64,128]{2,1,0:T(8,128)(2,1)S(1)}, u32[]{:S(2)}, u32[]{:S(2)}) async-start(bf16[64,64,128]{2,1,0:T(8,128)(2,1)} %broadcast_in_dim.10), calls=%async_computation.4 | async-start | bytes 2097152 | tf_op jit(solution)/shard_map/all_to_all | solution.py:11
  82.1 78.5 %copy-start.3 = (f32[64,128]{1,0:T(8,128)S(1)}, f32[64,128]{1,0:T(8,128)}, u32[]{:S(2)}) copy-start(f32[64,128]{1,0:T(8,128)} %param.9) | copy-start | bytes 98308
  121.8 38.9 %all-to-all-start.3 = ((bf16[64,128,64]{1,2,0:T(8,128)(2,1)}), bf16[64,128,64]{1,2,0:T(8,128)(2,1)}, u32[]{:S(2)}, u32[]{:S(2)}) async-start(bf16[64,128,64]{1,2,0:T(8,128)(2,1)} %stack.2), calls=%async_computation.3 | async-start | bytes 2097152 | tf_op jit(solution)/shard_map/all_to_all | solution.py:60
